TPU v7x, 32 devices: a whole 2x2x4 slice. The times are simulated.
32 devices in a mesh: vocab: 8 (over z, x), tok: 4 (over y, core).
Axes of the slice: x: 2, y: 2, z: 4, core: 2. Of those that a mesh axis runs over, the one named last changes fastest.
Arguments:
- hidden: bfloat16 [768, 7168], P('tok', 'vocab'), may hold values from -21 to 21
- head_weight: bfloat16 [7168, 8192], P('tok', 'vocab'), may hold values from -0.12695312 to 0.12695312
- targets: int32 [768], P('tok'), may hold values from 0 to 6143
- vocab_mask: int32 [8192], P('vocab'), may hold values from 0 to 1, as said below
- token_grad: float32 [768], P('tok'), may hold values from 16 to 160
Outputs:
- hidden_grad: bfloat16 [768, 7168], P('tok', 'vocab')
- token_loss: float32 [768], P('tok')
Inputs may be any that keep to these rules, and one draw needn't show every extreme that they name: vocab_mask is 1 on the columns below some cut and 0 from it on, with between 1 and 2048 zeros.
All inputs are finite; a program needn't handle non-finite values.
Results may differ from a plain program's by a relative error of at most 0.0051.
Values may be sent and summed in bfloat16 or wider, within the bound.
A program may use at most 64 MiB of HBM per device.

v0:
```python
import jax
import jax.numpy as jnp
from jax import lax
from jax.sharding import PartitionSpec as P


def combined_all(value, axis, join):
    pieces = jax.tree.map(lambda part: lax.all_gather(part, axis), value)
    head = jax.tree.map(lambda part: part[0], pieces)
    tail = jax.tree.map(lambda part: part[1:], pieces)
    running, _ = lax.scan(lambda running, share: (join(running, share), None), head, tail)
    return running


def combine_pairs(left_part, right_part):
    larger = jnp.maximum(left_part[0], right_part[0])
    summed = left_part[1] * jnp.exp(left_part[0] - larger) + right_part[1] * jnp.exp(
        right_part[0] - larger
    )
    return (larger, summed, left_part[2] + right_part[2])


def on_device(hidden, head_weight, targets, vocab_mask, token_grad):
    gathered = lax.all_gather(hidden, "vocab", axis=1, tiled=True)
    block_width = head_weight.shape[1]
    first_column = lax.axis_index("vocab") * block_width
    logits = jnp.dot(
        gathered,
        lax.all_gather(head_weight, "tok", axis=0, tiled=True),
        preferred_element_type=jnp.float32,
    )
    live_mask = vocab_mask[None, :] == 1
    masked = jnp.where(live_mask, logits, jnp.float32(-1e30))
    local_max = jnp.max(masked, axis=1)
    columns = first_column + jnp.arange(block_width, dtype=jnp.int32)
    onehot = columns[None, :] == targets[:, None]
    local_target = jnp.sum(jnp.where(onehot, logits, jnp.float32(0.0)), axis=1)
    local_sum = jnp.sum(jnp.exp(masked - local_max[:, None]), axis=1)
    row_max, denominator, target_logit = combined_all(
        (local_max, local_sum, local_target), "vocab", combine_pairs
    )
    log_norm = row_max + jnp.log(denominator)
    token_loss = log_norm - target_logit
    probabilities = jnp.exp(masked - log_norm[:, None])
    logit_grad = (token_grad[:, None] * (probabilities - onehot.astype(jnp.float32))).astype(
        jnp.bfloat16
    )
    partial_value = lax.dot_general(
        logit_grad,
        lax.all_gather(head_weight, "tok", axis=0, tiled=True),
        (((1,), (1,)), ((), ())),
        preferred_element_type=jnp.float32,
    )
    hidden_grad = lax.psum_scatter(partial_value, "vocab", scatter_dimension=1, tiled=True).astype(
        jnp.bfloat16
    )
    return (hidden_grad, token_loss)


def solution(mesh):
    placed = (P("tok", "vocab"), P("tok", "vocab"), P("tok"), P("vocab"), P("tok"))
    return jax.shard_map(
        on_device,
        mesh=mesh,
        in_specs=placed,
        out_specs=(P("tok", "vocab"), P("tok")),
        check_vma=False,
    )
```

profile of v0, /device:TPU:0, one launch (start us, length us, event | category | flops | bytes accessed | tf_op | source)
XLA Modules:
  0.0 334.8 jit_solution(9599591068299161233)
XLA Ops:
  7.2 0.7 all-gather.6.cloned.1.call-update
  7.9 0.7 all-gather.8.cloned.1.call-update
  8.7 0.0 reduce-scatter.2.cloned.1.call-start
  8.7 1.2 dynamic-slice
  10.6 0.7 broadcast_compare_fusion
  11.3 57.9 %all-gather.6.cloned.1.call-done = bf16[192,7168]{1,0:T(8,128)(2,1)} async-done(((bf16[192,896]{1,0:T(8,128)(2,1)}), bf16[192,7168]{1,0:T(8,128)(2,1)}) %all-gather.6.cloned.1.call-update) | async-done | bytes 2752528 | tf_op jit(solution)/shard_map/all_gather | solution.py:24
  69.2 93.7 %all-gather.8.cloned.1.call-done = bf16[7168,1024]{1,0:T(8,128)(2,1)} async-done(((bf16[1792,1024]{1,0:T(8,128)(2,1)}), bf16[7168,1024]{1,0:T(8,128)(2,1)}) %all-gather.8.cloned.1.call-update) | async-done | bytes 14680080 | tf_op jit(solution)/shard_map/all_gather | solution.py:29
  162.9 7.7 %select_reduce_fusion = (f32[192]{0:T(256)S(1)}, f32[192,1024]{1,0:T(8,128)S(1)}) fusion(pred[1024]{0:T(1024)(128)(4,1)S(1)} %broadcast_compare_fusion, bf16[192,7168]{1,0:T(8,128)(2,1)} %all-gather.6.cloned.1.call-done, bf16[7168,1024]{1,0:T(8,128)(2,1)} %all-gather.8.cloned.1.call-done), kind=kOutput, calls=%fused_computation.11 | convolution fusion | flops 2818965248 | bytes 18220800 | tf_op jit(solution)/shard_map/dot_general | solution.py:27
  170.6 0.3 dynamic-update-slice
  170.9 0.4 fusion
  171.3 0.3 dynamic-update-slice.1
  171.6 0.3 dynamic-update-slice.2
  171.8 37.0 %all-reduce.3 = (f32[1536]{0:T(1024)S(1)}, f32[1536]{0:T(1024)S(1)}, f32[1536]{0:T(1024)S(1)}) all-reduce(f32[1536]{0:T(1024)S(1)} %dynamic-update-slice, f32[1536]{0:T(1024)S(1)} %dynamic-update-slice.1, f32[1536]{0:T(1024)S(1)} %dynamic-update-slice.2), channel_id=2, replica_groups=mesh['vocab'=8,'tok'=4] {'vocab'}, use_global_device_ids=true, to_apply=%add | all-reduce | flops 4608 | bytes 36864
  208.8 0.1 slice.33
  208.9 0.1 slice.34
  209.0 0.1 slice.35
  209.0 0.1 reshape.23
  209.1 0.1 reshape.24
  209.2 0.1 reshape.25
  209.3 0.6 while.14
  209.8 0.6 fusion.13
  210.4 12.6 %fusion.4 = f32[192,7168]{1,0:T(8,128)} fusion(bf16[7168,1024]{1,0:T(8,128)(2,1)} %all-gather.8.cloned.1.call-done, f32[192,1024]{1,0:T(8,128)S(1)} %get-tuple-element.70, f32[192]{0:T(256)S(1)} %get-tuple-element.66, s32[1024]{0:T(1024)S(1)} %iota_add_fusion, f32[192]{0:T(256)S(1)} %copy-done.1, s32[192]{0:T(256)S(1)} %copy-done, ...), kind=kOutput, calls=%fused_computation.12 | convolution fusion | flops 2819948544 | bytes 20978944 | tf_op jit(solution)/shard_map/dot_general | solution.py:48
  223.0 103.4 %reduce-scatter.2.cloned.1.call-done = f32[192,896]{1,0:T(8,128)} async-done(((f32[192,7168]{1,0:T(8,128)}), f32[192,896]{1,0:T(8,128)}) %reduce-scatter.2.cloned.1.call-update) | async-done | bytes 688144 | tf_op jit(solution)/shard_map/reduce_scatter | solution.py:54
  326.4 1.9 convert_element_type.11
  (42 shorter events, 0.5 us)
Async XLA Ops:
  7.2 62.1 %all-gather.6.cloned.1.call-start = ((), (), s32[]{:S(2)}) async-start(), calls=%async_computation.1 | async-start | bytes 3096576 | tf_op jit(solution)/shard_map/all_gather | solution.py:24
  7.9 155.1 %all-gather.8.cloned.1.call-start = ((), (), s32[]{:S(2)}) async-start(), calls=%async_computation.2 | async-start | bytes 18350080 | tf_op jit(solution)/shard_map/all_gather | solution.py:29
  8.6 162.3 %copy-start = (s32[192]{0:T(256)S(1)}, s32[192]{0:T(256)}, u32[]{:S(2)}) copy-start(s32[192]{0:T(256)} %param.9) | copy-start | bytes 2308
  8.7 317.8 %reduce-scatter.2.cloned.1.call-start = ((), (), s32[]{:S(2)}) async-start(), calls=%async_computation.3 | async-start | bytes 6193152 | tf_op jit(solution)/shard_map/reduce_scatter | solution.py:54
  11.3 199.1 %copy-start.1 = (f32[192]{0:T(256)S(1)}, f32[192]{0:T(256)}, u32[]{:S(2)}) copy-start(f32[192]{0:T(256)} %param.11) | copy-start | bytes 2308
Sparse Core Ops, SparseCore 0:
  10.1 59.0 all-gather.5
  70.8 92.1 all-gather.7
  223.1 103.2 reduce-scatter.1
where the time goes:
time: 335 us
  waiting for transfers between devices  256 us (76%)
  blocking collectives  37 us (11%)
  matrix products  20.3 us (6%)
  between operations  14.5 us (4%)
  other arithmetic  3.74 us (1%)
    reduce_scatter x1, waiting for transfers between devices, on_device(): lax.psum_scatter(partial_value, 'vocab', scatter_dimension=1, tiled=True)  103 us
    all_gather x1, waiting for transfers between devices, on_device(): lax.all_gather(head_weight, 'tok', axis=0, tiled=True)  93.7 us
    all_gather x1, waiting for transfers between devices, on_device(): gathered = lax.all_gather(hidden, 'vocab', axis=1, tiled=True)  57.9 us
    unnamed x1, blocking collectives  37 us
    dot_general x1, matrix products, on_device(): lax.dot_general(logit_grad, lax.all_gather(head_weight, 'tok', axis=0, ti...  12.6 us
    dot_general x1, matrix products, on_device(): jnp.dot(gathered, lax.all_gather(head_weight, 'tok', axis=0, tiled=True),...  7.66 us
  transfers between devices with their start and end apart: 3, of which 3 were waited for; matrix products, arithmetic and copies ran while one was open for 1% of the time, Pallas kernels for 0%

commit v1 on v0

v1 whole, which is shorter than its diff:
```python
import jax
import jax.numpy as jnp
from jax import lax
from jax.sharding import PartitionSpec as P


def make_on_device(vocab_size, tok_size):
    share = vocab_size // tok_size
    moves = [
        (b * tok_size + a, (a * share + b % share) * tok_size + b // share)
        for a in range(tok_size)
        for b in range(vocab_size)
    ]
    back = [(there, here) for here, there in moves]

    def on_device(hidden, head_weight, targets, vocab_mask, token_grad):
        rows, feats = hidden.shape
        block_width = head_weight.shape[1]
        moved = lax.ppermute(hidden, ("vocab", "tok"), moves)
        pieces = lax.all_gather(moved, "vocab")
        gathered = (
            pieces.reshape(tok_size, share, rows, feats)
            .transpose(0, 2, 1, 3)
            .reshape(tok_size * rows, share * feats)
        )
        partial_logits = jnp.dot(gathered, head_weight, preferred_element_type=jnp.float32)
        logits = lax.psum_scatter(partial_logits, "tok", scatter_dimension=0, tiled=True)
        first_column = lax.axis_index("vocab") * block_width
        masked = jnp.where(vocab_mask[None, :] == 1, logits, jnp.float32(-1e30))
        local_max = jnp.max(masked, axis=1)
        columns = first_column + jnp.arange(block_width, dtype=jnp.int32)
        onehot = columns[None, :] == targets[:, None]
        local_target = jnp.sum(jnp.where(onehot, logits, jnp.float32(0.0)), axis=1)
        weights = jnp.exp(masked - local_max[:, None])
        local_sum = jnp.sum(weights, axis=1)
        stats = lax.all_gather(jnp.stack([local_max, local_sum, local_target]), "vocab")
        row_max = jnp.max(stats[:, 0], axis=0)
        denominator = jnp.sum(stats[:, 1] * jnp.exp(stats[:, 0] - row_max[None]), axis=0)
        target_logit = jnp.sum(stats[:, 2], axis=0)
        log_norm = row_max + jnp.log(denominator)
        token_loss = log_norm - target_logit
        probabilities = jnp.exp(masked - log_norm[:, None])
        logit_grad = (
            token_grad[:, None] * (probabilities - onehot.astype(jnp.float32))
        ).astype(jnp.bfloat16)
        all_grads = lax.all_gather(logit_grad, "tok", axis=0, tiled=True)
        partial_value = lax.dot_general(
            all_grads,
            head_weight,
            (((1,), (1,)), ((), ())),
            preferred_element_type=jnp.float32,
        )
        blocks = (
            partial_value.reshape(tok_size, rows, share, feats)
            .transpose(0, 2, 1, 3)
            .reshape(vocab_size, rows, feats)
        )
        summed = lax.psum_scatter(blocks, "vocab", scatter_dimension=0, tiled=False)
        hidden_grad = lax.ppermute(summed.astype(jnp.bfloat16), ("vocab", "tok"), back)
        return (hidden_grad, token_loss)

    return on_device


def solution(mesh):
    placed = (P("tok", "vocab"), P("tok", "vocab"), P("tok"), P("vocab"), P("tok"))
    return jax.shard_map(
        make_on_device(mesh.shape["vocab"], mesh.shape["tok"]),
        mesh=mesh,
        in_specs=placed,
        out_specs=(P("tok", "vocab"), P("tok")),
        check_vma=False,
    )
```

time: 335 us -> 347 us (1.036)
  the two profiles are of different devices: /device:TPU:0 before, /device:TPU:4 now
where the time goes in v1:
time: 347 us
  waiting for transfers between devices  252 us (73%)
  blocking collectives  30.9 us (9%)
  local copies, waits for them, and re-layouts  21.9 us (6%)
  between operations  13.8 us (4%)
  matrix products  12.6 us (4%)
  starting transfers between devices  8.3 us (2%)
  other arithmetic  6.71 us (2%)
    reduce_scatter x1, waiting for transfers between devices, on_device(): summed = lax.psum_scatter(blocks, 'vocab', scatter_dimension=0, tiled=False)  109 us
    all_gather x1, waiting for transfers between devices, on_device(): pieces = lax.all_gather(moved, 'vocab')  54.7 us
    reduce_scatter x1, waiting for transfers between devices, on_device(): lax.psum_scatter(partial_logits, 'tok', scatter_dimension=0, tiled=True)  34.8 us
    all_gather x1, blocking collectives, on_device(): lax.all_gather(jnp.stack([local_max, local_sum, local_target]), 'vocab')  30.9 us
    all_gather x1, waiting for transfers between devices, on_device(): all_grads = lax.all_gather(logit_grad, 'tok', axis=0, tiled=True)  19.5 us
    ppermute x1, waiting for transfers between devices, on_device(): lax.ppermute(summed.astype(jnp.bfloat16), ('vocab', 'tok'), back)  17.4 us
    ppermute x1, waiting for transfers between devices, on_device(): moved = lax.ppermute(hidden, ('vocab', 'tok'), moves)  17.3 us
    dot_general x1, matrix products, on_device(): lax.dot_general(all_grads, head_weight, (((1,), (1,)), ((), ())), preferr...  7.95 us
  transfers between devices with their start and end apart: 6, of which 6 were waited for; matrix products, arithmetic and copies ran while one was open for 0% of the time, Pallas kernels for 0%

profile of v1, /device:TPU:4, one launch (start us, length us, event | category | flops | bytes accessed | tf_op | source)
XLA Modules:
  0.0 346.6 jit_solution(7393957762634626419)
XLA Ops:
  7.2 4.4 %collective-permute-start = (bf16[192,896]{1,0:T(8,128)(2,1)}, bf16[192,896]{1,0:T(8,128)(2,1)S(1)}, u32[]{:S(2)}, u32[]{:S(2)}) collective-permute-start(bf16[192,896]{1,0:T(8,128)(2,1)} %param.5), channel_id=1, source_target_pairs={{0,0},{4,4},{8,1},{12,5},{16,2},{20,6},{24,3},{28,7},{1,8},{5,12},... | collective-permute-start | bytes 1032200 | tf_op jit(solution)/shard_map/ppermute | solution.py:19
  11.7 17.3 %collective-permute-done = bf16[192,896]{1,0:T(8,128)(2,1)S(1)} collective-permute-done((bf16[192,896]{1,0:T(8,128)(2,1)}, bf16[192,896]{1,0:T(8,128)(2,1)S(1)}, u32[]{:S(2)}, u32[]{:S(2)}) %collective-permute-start) | collective-permute-done | bytes 344096 | tf_op jit(solution)/shard_map/ppermute | solution.py:19
  29.0 0.7 copy-done
  29.8 54.7 %all-gather.8.cloned.1.call-done = bf16[1536,896]{1,0:T(8,128)(2,1)} async-done(((bf16[192,896]{1,0:T(8,128)(2,1)}), bf16[1536,896]{1,0:T(8,128)(2,1)}) %all-gather.8.cloned.1.call-update) | async-done | bytes 2752528 | tf_op jit(solution)/shard_map/all_gather | solution.py:20
  84.5 4.6 %copy.12 = bf16[4,2,192,896]{3,1,2,0:T(2,128)(2,1)S(1)} copy(bf16[4,2,192,896]{3,2,1,0:T(8,128)(2,1)} %bitcast.33) | data formatting | bytes 5505024 | tf_op jit(solution)/shard_map/reshape | solution.py:22
  89.1 0.5 copy.18
  89.6 1.5 copy-done.4
  91.1 4.7 %fusion.10 = f32[768,1024]{1,0:T(8,128)} fusion(bf16[768,1792]{1,0:T(8,128)(2,1)S(1)} %bitcast.34, bf16[1792,1024]{1,0:T(8,128)(2,1)S(1)} %copy-done.4), kind=kOutput, calls=%fused_computation.22 | convolution fusion | flops 2818572288 | bytes 9568256 | tf_op jit(solution)/shard_map/dot_general | solution.py:26
  95.9 0.6 copy-done.2
  96.5 34.8 %reduce-scatter.3.cloned.1.call-done = f32[192,1024]{1,0:T(8,128)} async-done(((f32[768,1024]{1,0:T(8,128)}), f32[192,1024]{1,0:T(8,128)}) %reduce-scatter.3.cloned.1.call-update) | async-done | bytes 786448 | tf_op jit(solution)/shard_map/reduce_scatter | solution.py:27
  131.3 1.3 select_reduce_fusion
  132.6 1.5 exponential_reduce_fusion
  134.1 30.9 %all-gather.2 = f32[8,3,192]{2,1,0:T(4,128)S(1)} all-gather(f32[1,3,192]{2,1,0:T(4,128)S(1)} %maximum_bitcast_fusion), channel_id=3, replica_groups=mesh['vocab'=8,'tok'=4] {'vocab'}, dimensions={0}, use_global_device_ids=true | all-gather | bytes 20736 | tf_op jit(solution)/shard_map/all_gather | solution.py:36
  165.0 0.6 fusion.8
  165.6 2.2 fusion.3
  167.9 19.5 %all-gather.6.cloned.1.call-done = bf16[768,1024]{1,0:T(8,128)(2,1)} async-done(((bf16[192,1024]{1,0:T(8,128)(2,1)}), bf16[768,1024]{1,0:T(8,128)(2,1)}) %all-gather.6.cloned.1.call-update) | async-done | bytes 1572880 | tf_op jit(solution)/shard_map/all_gather | solution.py:46
  187.4 7.9 %fusion.11 = f32[768,1792]{1,0:T(8,128)} fusion(bf16[768,1024]{1,0:T(8,128)(2,1)} %all-gather.6.cloned.1.call-done, bf16[1792,1024]{1,0:T(8,128)(2,1)} %param.6), kind=kOutput, calls=%fused_computation.23 | convolution fusion | flops 2818572288 | bytes 10747904 | tf_op jit(solution)/shard_map/dot_general | solution.py:47
  195.3 7.8 %reshape.35 = f32[4,192,2,896]{3,2,1,0:T(2,128)} reshape(f32[768,1792]{1,0:T(8,128)} %fusion.11) | data formatting | bytes 11010048 | tf_op jit(solution)/shard_map/reshape | solution.py:54
  203.1 5.3 %copy.14 = f32[4,2,192,896]{3,2,1,0:T(8,128)} copy(f32[4,2,192,896]{3,1,2,0:T(2,128)} %bitcast.31) | data formatting | bytes 11010048 | tf_op jit(solution)/shard_map/transpose | solution.py:55
  208.5 108.6 %reduce-scatter.5.cloned.1.call-done = f32[1,192,896]{2,1,0:T(8,128)} async-done(((f32[8,192,896]{2,1,0:T(8,128)}), f32[1,192,896]{2,1,0:T(8,128)}) %reduce-scatter.5.cloned.1.call-update) | async-done | bytes 688144 | tf_op jit(solution)/shard_map/reduce_scatter | solution.py:58
  317.1 1.1 convert_bitcast_fusion
  318.2 3.7 %collective-permute-start.1 = (bf16[192,896]{1,0:T(8,128)(2,1)S(1)}, bf16[192,896]{1,0:T(8,128)(2,1)S(1)}, u32[]{:S(2)}, u32[]{:S(2)}) collective-permute-start(bf16[192,896]{1,0:T(8,128)(2,1)S(1)} %convert_bitcast_fusion), channel_id=1, source_target_pairs={{0,0},{4,4},{1,8},{5,12},{2,16},{6,20},{3,24},{7,28},{8,1},{12,5},... | collective-permute-start | bytes 1032200 | tf_op jit(solution)/shard_map/ppermute | solution.py:59
  321.9 17.4 %collective-permute-done.1 = bf16[192,896]{1,0:T(8,128)(2,1)S(1)} collective-permute-done((bf16[192,896]{1,0:T(8,128)(2,1)S(1)}, bf16[192,896]{1,0:T(8,128)(2,1)S(1)}, u32[]{:S(2)}, u32[]{:S(2)}) %collective-permute-start.1) | collective-permute-done | bytes 344096 | tf_op jit(solution)/shard_map/ppermute | solution.py:59
  339.4 0.7 copy.30
  (20 shorter events, 0.3 us)
Async XLA Ops:
  7.2 77.3 %all-gather.8.cloned.1.call-start = ((), (), s32[]{:S(2)}) async-start(), calls=%async_computation.5 | async-start | bytes 3096576 | tf_op jit(solution)/shard_map/all_gather | solution.py:20
  7.2 21.8 %collective-permute-start = (bf16[192,896]{1,0:T(8,128)(2,1)}, bf16[192,896]{1,0:T(8,128)(2,1)S(1)}, u32[]{:S(2)}, u32[]{:S(2)}) collective-permute-start(bf16[192,896]{1,0:T(8,128)(2,1)} %param.5), channel_id=1, source_target_pairs={{0,0},{4,4},{8,1},{12,5},{16,2},{20,6},{24,3},{28,7},{1,8},{5,12},... | collective-permute-start | bytes 1032200 | tf_op jit(solution)/shard_map/ppermute | solution.py:19
  29.0 0.7 copy-start
  29.7 101.6 %reduce-scatter.3.cloned.1.call-start = ((), (), s32[]{:S(2)}) async-start(), calls=%async_computation.2 | async-start | bytes 3932160 | tf_op jit(solution)/shard_map/reduce_scatter | solution.py:27
  89.1 2.0 copy-start.4
  95.8 0.7 copy-start.2
  95.8 36.8 %copy-start.1 = (s32[192]{0:T(256)S(1)}, s32[192]{0:T(256)}, u32[]{:S(2)}) copy-start(s32[192]{0:T(256)} %param.7) | copy-start | bytes 2308
  95.8 69.8 %copy-start.3 = (f32[192]{0:T(256)S(1)}, f32[192]{0:T(256)}, u32[]{:S(2)}) copy-start(f32[192]{0:T(256)} %param.9) | copy-start | bytes 2308
  95.8 91.5 %all-gather.6.cloned.1.call-start = ((), (), s32[]{:S(2)}) async-start(), calls=%async_computation.3 | async-start | bytes 1966080 | tf_op jit(solution)/shard_map/all_gather | solution.py:46
  167.8 149.3 %reduce-scatter.5.cloned.1.call-start = ((), (), s32[]{:S(2)}) async-start(), calls=%async_computation.4 | async-start | bytes 6193152 | tf_op jit(solution)/shard_map/reduce_scatter | solution.py:58
  318.2 21.2 %collective-permute-start.1 = (bf16[192,896]{1,0:T(8,128)(2,1)S(1)}, bf16[192,896]{1,0:T(8,128)(2,1)S(1)}, u32[]{:S(2)}, u32[]{:S(2)}) collective-permute-start(bf16[192,896]{1,0:T(8,128)(2,1)S(1)} %convert_bitcast_fusion), channel_id=1, source_target_pairs={{0,0},{4,4},{1,8},{5,12},{2,16},{6,20},{3,24},{7,28},{8,1},{12,5},... | collective-permute-start | bytes 1032200 | tf_op jit(solution)/shard_map/ppermute | solution.py:59
Sparse Core Ops, SparseCore 0:
  29.8 54.5 all-gather.7
  95.9 35.3 reduce-scatter.2
  167.9 19.3 all-gather.5
  208.6 108.4 reduce-scatter.4

commit v2 on v1

--- a/solution.py
+++ b/solution.py
@@ -1,6 +1,8 @@
 import jax
 import jax.numpy as jnp
 from jax import lax
+from jax.experimental import pallas as pl
+from jax.experimental.pallas import tpu as pltpu
 from jax.sharding import PartitionSpec as P
 
 
@@ -62,10 +64,420 @@
     return on_device
 
 
+CHUNKS = 2
+BF = jnp.bfloat16
+F32 = jnp.float32
+
+
+def kernel(
+    depth,
+    hidden_ref, weight_ref, targets_ref, mask_ref, grad_ref,
+    out_ref, loss_ref,
+    gath, hb, plog, pair_in, cross_in, cross_out, dl, stats_out, stats_in,
+    term_out, term_in, up_in, down_in, up_out, down_out, far_out, far_in,
+    load_sem, x_send, x_recv, zu_send, zu_recv, zd_send, zd_recv, t_send, t_recv,
+    p_send, p_recv, c_send, c_recv, s_send, s_recv, g_send, g_recv,
+    e_send, e_recv, eu_send, eu_recv, ed_send, ed_recv, f_send, f_recv,
+):
+    rows, feats = hidden_ref.shape
+    part = rows // CHUNKS
+    width = weight_ref.shape[1]
+    me_v = lax.axis_index("vocab")
+    me_t = lax.axis_index("tok")
+    z, x = me_v // 2, me_v % 2
+    y, c = me_t // 2, me_t % 2
+    nv = 2 * depth
+
+    def dev(v, t):
+        return {"vocab": v, "tok": t}
+
+    def tok_of(r):
+        return ((y + r // 2) % 2) * 2 + (c + r % 2) % 2
+
+    other_x = z * 2 + (1 - x)
+
+    def rcopy(src, dst, ss, rs, v, t):
+        return pltpu.make_async_remote_copy(
+            src_ref=src, dst_ref=dst, send_sem=ss, recv_sem=rs,
+            device_id=dev(v, t), device_id_type=pl.DeviceIdType.MESH,
+        )
+
+    def span(h):
+        return pl.ds(h * part, part)
+
+    loads = [
+        pltpu.make_async_copy(hidden_ref.at[span(h)], gath.at[0, z, h], load_sem.at[h])
+        for h in range(CHUNKS)
+    ]
+    for load in loads:
+        load.start()
+
+    barrier = pltpu.get_barrier_semaphore()
+    for r in range(1, 4):
+        pl.semaphore_signal(barrier, inc=1, device_id=dev(me_v, tok_of(r)), device_id_type=pl.DeviceIdType.MESH)
+    for k in range(1, nv):
+        pl.semaphore_signal(barrier, inc=1, device_id=dev((me_v + k) % nv, me_t), device_id_type=pl.DeviceIdType.MESH)
+    pl.semaphore_wait(barrier, 3 + nv - 1)
+
+    def x_copy(h):
+        return rcopy(gath.at[0, z, h], gath.at[1, z, h], x_send.at[h], x_recv.at[h], other_x, me_t)
+
+    def up_copy(q, zz, h):
+        return rcopy(gath.at[q, zz, h], gath.at[q, zz, h], zu_send.at[q, zz, h], zu_recv.at[q, zz, h], me_v + 2, me_t)
+
+    def down_copy(q, zz, h):
+        return rcopy(gath.at[q, zz, h], gath.at[q, zz, h], zd_send.at[q, zz, h], zd_recv.at[q, zz, h], me_v - 2, me_t)
+
+    def rel(zz):
+        return 2 * ((zz // 2 + y) % 2) + (zz % 2 + c) % 2
+
+    def t_copy(q, zz, h):
+        r = rel(zz)
+        return rcopy(gath.at[q, zz, h], hb.at[q, r, h], t_send.at[q, zz, h], t_recv.at[q, r, h], me_v, zz)
+
+    def pass_on(q, zz, h):
+        @pl.when(zz != me_t)
+        def _():
+            t_copy(q, zz, h).start()
+
+    for h in range(CHUNKS):
+        loads[h].wait()
+        x_copy(h).start()
+    for s in range(depth):
+        for h in range(CHUNKS):
+            for q in range(2):
+                if s == 0:
+                    if q == 1:
+                        x_copy(h).wait_recv()
+
+                    @pl.when(z < depth - 1)
+                    def _():
+                        up_copy(q, z, h).start()
+
+                    @pl.when(z > 0)
+                    def _():
+                        down_copy(q, z, h).start()
+
+                    pass_on(q, z, h)
+                else:
+                    @pl.when(z - s >= 0)
+                    def _():
+                        up_copy(q, z - s, h).wait_recv()
+
+                        @pl.when(z < depth - 1)
+                        def _():
+                            up_copy(q, z - s, h).start()
+
+                        pass_on(q, z - s, h)
+
+                    @pl.when(z + s < depth)
+                    def _():
+                        down_copy(q, z + s, h).wait_recv()
+
+                        @pl.when(z > 0)
+                        def _():
+                            down_copy(q, z + s, h).start()
+
+                        pass_on(q, z + s, h)
+
+    for q in range(2):
+        for h in range(CHUNKS):
+            hb[q, 0, h] = gath[q, me_t, h]
+
+    def weight_rows(q):
+        owner = (x + q) % 2
+        return pl.ds(pl.multiple_of(owner * feats, 128), feats)
+
+    tile = 256
+
+    def logits_of(r0, nr):
+        @pl.loop(0, width // tile)
+        def _(j):
+            cols = pl.ds(pl.multiple_of(j * tile, tile), tile)
+            total = None
+            for q in range(2):
+                lhs = hb[q, pl.ds(r0, nr)].reshape(nr * rows, feats)
+                term = jnp.dot(lhs, weight_ref[weight_rows(q), cols], preferred_element_type=F32)
+                total = term if total is None else total + term
+            plog[pl.ds(r0, nr), :, cols] = total.reshape(nr, rows, tile)
+
+    def pair_copy(k):
+        return rcopy(plog.at[1 + 2 * k], pair_in.at[k], p_send.at[k], p_recv.at[k], me_v, tok_of(1))
+
+    def cross_copy():
+        return rcopy(cross_out, cross_in, c_send.at[0], c_recv.at[0], me_v, tok_of(2))
+
+    def await_rel(r):
+        for q in range(2):
+            for h in range(CHUNKS):
+                rcopy(gath.at[q, 0, h], hb.at[q, r, h], t_send.at[q, 0, h], t_recv.at[q, r, h], me_v, tok_of(1)).wait_recv()
+
+    await_rel(2)
+    await_rel(3)
+    logits_of(2, 2)
+    pair_copy(1).start()
+    await_rel(1)
+    logits_of(0, 2)
+    pair_copy(0).start()
+    pair_copy(1).wait_recv()
+    cross_out[...] = plog[2] + pair_in[1]
+    cross_copy().start()
+    pair_copy(0).wait_recv()
+    plog[0] = plog[0] + pair_in[0]
+    cross_copy().wait_recv()
+    logits = plog[0] + cross_in[...]
+
+    masked = jnp.where(mask_ref[...] == 1, logits, jnp.float32(-1e30))
+    local_max = jnp.max(masked, axis=1, keepdims=True)
+    columns = me_v * width + lax.broadcasted_iota(jnp.int32, (rows, width), 1)
+    onehot = columns == targets_ref[...]
+    local_target = jnp.sum(jnp.where(onehot, logits, 0.0), axis=1, keepdims=True)
+    local_sum = jnp.sum(jnp.exp(masked - local_max), axis=1, keepdims=True)
+    lanes = lax.broadcasted_iota(jnp.int32, (rows, 128), 1)
+    packed = jnp.where(lanes == 0, local_max, jnp.where(lanes == 1, local_sum, local_target))
+    tall = jnp.concatenate([packed, jnp.zeros((256 - rows, 128), F32)], axis=0)
+    mine = jnp.transpose(tall)[0:8]
+    stats_out[...] = mine
+    stats_in[me_v] = mine
+    plog[0] = masked
+
+    def stat_copy(k):
+        return rcopy(stats_out, stats_in.at[me_v], s_send.at[k], s_recv.at[me_v], (me_v + k) % nv, me_t)
+
+    for k in range(1, nv):
+        stat_copy(k).start()
+    for k in range(1, nv):
+        source = (me_v + nv - k) % nv
+        rcopy(stats_out, stats_in.at[source], s_send.at[k], s_recv.at[source], source, me_t).wait_recv()
+    row_max = stats_in[0][0:1]
+    for v in range(1, nv):
+        row_max = jnp.maximum(row_max, stats_in[v][0:1])
+    denominator = jnp.zeros_like(row_max)
+    target_logit = jnp.zeros_like(row_max)
+    for v in range(nv):
+        got = stats_in[v]
+        denominator += got[1:2] * jnp.exp(got[0:1] - row_max)
+        target_logit += got[2:3]
+    log_norm = row_max + jnp.log(denominator)
+    loss_ref[...] = jnp.broadcast_to(log_norm - target_logit, loss_ref.shape)
+    column = jnp.transpose(jnp.broadcast_to(log_norm, (128, 256)))[0:rows, 0:1]
+    probabilities = jnp.exp(plog[0] - column)
+    dl[0] = (grad_ref[...] * (probabilities - onehot.astype(F32))).astype(BF)
+
+    def grad_copy(i):
+        if i == 0:
+            return rcopy(dl.at[0], dl.at[2], g_send.at[0], g_recv.at[0], me_v, tok_of(2))
+        if i == 1:
+            return rcopy(dl.at[0], dl.at[1], g_send.at[1], g_recv.at[1], me_v, tok_of(1))
+        return rcopy(dl.at[2], dl.at[3], g_send.at[2], g_recv.at[2], me_v, tok_of(1))
+
+    grad_copy(0).start()
+    grad_copy(1).start()
+
+    def term_copy(q, r, h):
+        return rcopy(
+            term_out.at[q, r, h], term_in.at[q, me_t, h], e_send.at[q, r, h], e_recv.at[q, r, h], me_v, tok_of(r)
+        )
+
+    def terms_of(q, r0):
+        lhs = dl[pl.ds(r0, 2)].reshape(2 * rows, width)
+        value = lax.dot_general(
+            lhs, weight_ref[weight_rows(q), :], (((1,), (1,)), ((), ())), preferred_element_type=F32
+        ).astype(BF).reshape(2, CHUNKS, part, feats)
+        for i in range(2):
+            if r0 + i == 0:
+                term_in[q, me_t] = value[0]
+            else:
+                term_out[q, r0 + i] = value[i]
+
+    grad_copy(1).wait_recv()
+    for q in (1, 0):
+        terms_of(q, 0)
+    grad_copy(0).wait_recv()
+    grad_copy(2).start()
+    grad_copy(2).wait_recv()
+    for q in (1, 0):
+        terms_of(q, 2)
+        for h in range(CHUNKS):
+            for r in (2, 3, 1):
+                term_copy(q, r, h).start()
+
+    def eu_copy(q, zz, h):
+        return rcopy(up_out.at[q, zz, h], up_in.at[q, zz, h], eu_send.at[q, zz, h], eu_recv.at[q, zz, h], me_v + 2, me_t)
+
+    def ed_copy(q, zz, h):
+        return rcopy(down_out.at[q, zz, h], down_in.at[q, zz, h], ed_send.at[q, zz, h], ed_recv.at[q, zz, h], me_v - 2, me_t)
+
+    def far_copy(h):
+        return rcopy(far_out.at[h], far_in.at[h], f_send.at[h], f_recv.at[h], other_x, me_t)
+
+    for q in (1, 0):
+        for h in range(CHUNKS):
+            for r in (1, 2, 3):
+                rcopy(term_out.at[q, r, h], term_in.at[q, tok_of(r), h], e_send.at[q, r, h], e_recv.at[q, r, h], me_v, tok_of(r)).wait_recv()
+            for k in range(depth - 1, 0, -1):
+                @pl.when(z + k < depth)
+                def _():
+                    zz = z + k
+
+                    @pl.when(z > 0)
+                    def _():
+                        eu_copy(q, zz, h).wait_recv()
+                        up_out[q, zz, h] = (
+                            term_in[q, zz, h].astype(F32) + up_in[q, zz, h].astype(F32)
+                        ).astype(BF)
+
+                    @pl.when(z == 0)
+                    def _():
+                        up_out[q, zz, h] = term_in[q, zz, h]
+
+                    eu_copy(q, zz, h).start()
+
+                @pl.when(z - k >= 0)
+                def _():
+                    zz = z - k
+
+                    @pl.when(z < depth - 1)
+                    def _():
+                        ed_copy(q, zz, h).wait_recv()
+                        down_out[q, zz, h] = (
+                            term_in[q, zz, h].astype(F32) + down_in[q, zz, h].astype(F32)
+                        ).astype(BF)
+
+                    @pl.when(z == depth - 1)
+                    def _():
+                        down_out[q, zz, h] = term_in[q, zz, h]
+
+                    ed_copy(q, zz, h).start()
+
+    for q in (1, 0):
+        for h in range(CHUNKS):
+            @pl.when(z > 0)
+            def _():
+                eu_copy(q, z, h).wait_recv()
+
+            @pl.when(z < depth - 1)
+            def _():
+                ed_copy(q, z, h).wait_recv()
+
+            def total():
+                own = term_in[q, z, h].astype(F32)
+                below = jnp.where(z > 0, up_in[q, z, h].astype(F32), 0.0)
+                above = jnp.where(z < depth - 1, down_in[q, z, h].astype(F32), 0.0)
+                return own + below + above
+
+            if q == 1:
+                far_out[h] = total().astype(BF)
+                far_copy(h).start()
+            else:
+                far_copy(h).wait_recv()
+                out_ref[span(h), :] = (total() + far_in[h].astype(F32)).astype(BF)
+
+    for h in range(CHUNKS):
+        x_copy(h).wait_send()
+        far_copy(h).wait_send()
+        for q in range(2):
+            for s in range(depth):
+                @pl.when(z - s >= 0)
+                def _():
+                    @pl.when(z < depth - 1)
+                    def _():
+                        up_copy(q, z - s, h).wait_send()
+
+                @pl.when(z + s < depth)
+                def _():
+                    @pl.when(z > 0)
+                    def _():
+                        down_copy(q, z + s, h).wait_send()
+
+                @pl.when(me_t != s)
+                def _():
+                    t_copy(q, s, h).wait_send()
+
+            for k in range(1, depth):
+                @pl.when(z + k < depth)
+                def _():
+                    eu_copy(q, z + k, h).wait_send()
+
+                @pl.when(z - k >= 0)
+                def _():
+                    ed_copy(q, z - k, h).wait_send()
+
+            for r in range(1, 4):
+                term_copy(q, r, h).wait_send()
+    for k in range(2):
+        pair_copy(k).wait_send()
+    cross_copy().wait_send()
+    for k in range(1, nv):
+        stat_copy(k).wait_send()
+    for i in range(3):
+        grad_copy(i).wait_send()
+
+
+def fused(vocab_size, tok_size):
+    depth = vocab_size // 2
+
+    def on_device(hidden, head_weight, targets, vocab_mask, token_grad):
+        rows, feats = hidden.shape
+        width = head_weight.shape[1]
+        part = rows // CHUNKS
+        dma = pltpu.SemaphoreType.DMA
+        block = (CHUNKS, part, feats)
+        by_q = (2, depth, CHUNKS)
+        vmem = pl.BlockSpec(memory_space=pltpu.VMEM)
+        hidden_grad, loss = pl.pallas_call(
+            lambda *refs: kernel(depth, *refs),
+            out_shape=(
+                jax.ShapeDtypeStruct((rows, feats), BF),
+                jax.ShapeDtypeStruct((8, 256), F32),
+            ),
+            in_specs=[pl.BlockSpec(memory_space=pltpu.HBM)] + [vmem] * 4,
+            out_specs=(vmem, vmem),
+            scratch_shapes=[
+                pltpu.VMEM((2, depth) + block, BF),
+                pltpu.VMEM((2, 4) + block, BF),
+                pltpu.VMEM((4, rows, width), F32),
+                pltpu.VMEM((2, rows, width), F32),
+                pltpu.VMEM((rows, width), F32),
+                pltpu.VMEM((rows, width), F32),
+                pltpu.VMEM((4, rows, width), BF),
+                pltpu.VMEM((8, 256), F32),
+                pltpu.VMEM((vocab_size, 8, 256), F32),
+                pltpu.VMEM((2, 4) + block, BF),
+                pltpu.VMEM((2, 4) + block, BF),
+                pltpu.VMEM((2, depth) + block, BF),
+                pltpu.VMEM((2, depth) + block, BF),
+                pltpu.VMEM((2, depth) + block, BF),
+                pltpu.VMEM((2, depth) + block, BF),
+                pltpu.VMEM(block, BF),
+                pltpu.VMEM(block, BF),
+                dma((CHUNKS,)), dma((CHUNKS,)), dma((CHUNKS,)),
+                dma(by_q), dma(by_q), dma(by_q), dma(by_q), dma(by_q), dma(by_q),
+                dma((2,)), dma((2,)), dma((1,)), dma((1,)),
+                dma((vocab_size,)), dma((vocab_size,)), dma((3,)), dma((3,)),
+                dma(by_q), dma(by_q), dma(by_q), dma(by_q), dma(by_q), dma(by_q),
+                dma((CHUNKS,)), dma((CHUNKS,)),
+            ],
+            compiler_params=pltpu.CompilerParams(
+                collective_id=0, has_side_effects=True, vmem_limit_bytes=60 * 1024 * 1024
+            ),
+        )(hidden, head_weight, targets[:, None], vocab_mask[None, :], token_grad[:, None])
+        return (hidden_grad, loss[0, :rows])
+
+    return on_device
+
+
 def solution(mesh):
     placed = (P("tok", "vocab"), P("tok", "vocab"), P("tok"), P("vocab"), P("tok"))
+    vocab_size, tok_size = mesh.shape["vocab"], mesh.shape["tok"]
+
+    def body(hidden, *rest):
+        fits = tok_size == 4 and vocab_size == 2 * tok_size and hidden.shape[1] % 128 == 0
+        build = fused if fits and hidden.shape[0] <= 256 else make_on_device
+        return build(vocab_size, tok_size)(hidden, *rest)
+
     return jax.shard_map(
-        make_on_device(mesh.shape["vocab"], mesh.shape["tok"]),
+        body,
         mesh=mesh,
         in_specs=placed,
         out_specs=(P("tok", "vocab"), P("tok")),

time: 347 us -> 167 us (0.48)
  the two profiles are of different devices: /device:TPU:4 before, /device:TPU:0 now
where the time goes in v2:
time: 167 us
  Pallas kernels  161 us (96%)
  local copies, waits for them, and re-layouts  5.88 us (4%)
    pallas_call x1, Pallas kernels, on_device(): pl.pallas_call(lambda *refs: kernel(depth, *refs), out_shape=(jax.ShapeDt...  161 us

profile of v2, /device:TPU:0, one launch (start us, length us, event | category | flops | bytes accessed | tf_op | source)
XLA Modules:
  0.0 167.1 jit_solution(1781691247198763324)
XLA Ops:
  0.6 1.4 copy.7.refs_2_
  2.1 1.4 copy.8.refs_4_
  3.5 160.5 %shard_map.68 = (bf16[192,896]{1,0:T(8,128)(2,1)}, f32[8,256]{1,0:T(8,128)}) custom-call(bf16[192,896]{1,0:T(8,128)(2,1)} %refs_0_.1, bf16[1792,1024]{1,0:T(8,128)(2,1)} %refs_1_.1, s32[192,1]{1,0:T(8,128)} %copy.7.refs_2_, s32[1,1024]{1,0:T(1,128)} %bitcast.4, f32[192,1]{1,0:T(8,128)} %copy.8.refs_4_), custom_call_target="tpu_custom_call" | custom-call | tf_op jit(solution)/shard_map/pallas_call | solution.py:428
  164.1 1.3 slice.3
  165.3 1.7 %copy.10 = bf16[192,896]{1,0:T(8,128)(2,1)} copy(bf16[192,896]{1,0:T(8,128)(2,1)} %get-tuple-element.8) | data formatting | bytes 688128

commit v3 on v2

--- a/solution.py
+++ b/solution.py
@@ -64,7 +64,10 @@
     return on_device
 
 
-CHUNKS = 2
+CHUNKS = 3
+LATE = (0, 1)
+EARLY = (2,)
+ORDER = LATE + EARLY
 BF = jnp.bfloat16
 F32 = jnp.float32
 
@@ -74,10 +77,10 @@
     hidden_ref, weight_ref, targets_ref, mask_ref, grad_ref,
     out_ref, loss_ref,
     gath, hb, plog, pair_in, cross_in, cross_out, dl, stats_out, stats_in,
-    term_out, term_in, up_in, down_in, up_out, down_out, far_out, far_in,
+    term_out, term_in, up_in, down_in, up_out, down_out, far_out, far_in, near, mix_out, mix_in,
     load_sem, x_send, x_recv, zu_send, zu_recv, zd_send, zd_recv, t_send, t_recv,
     p_send, p_recv, c_send, c_recv, s_send, s_recv, g_send, g_recv,
-    e_send, e_recv, eu_send, eu_recv, ed_send, ed_recv, f_send, f_recv,
+    e_send, e_recv, eu_send, eu_recv, ed_send, ed_recv, f_send, f_recv, w_send, w_recv, m_send, m_recv,
 ):
     rows, feats = hidden_ref.shape
     part = rows // CHUNKS
@@ -119,6 +122,12 @@
         pl.semaphore_signal(barrier, inc=1, device_id=dev((me_v + k) % nv, me_t), device_id_type=pl.DeviceIdType.MESH)
     pl.semaphore_wait(barrier, 3 + nv - 1)
 
+    top = jnp.concatenate([targets_ref[...].astype(F32), grad_ref[...]], axis=0)
+    top = jnp.concatenate([top, jnp.zeros((2, 256 - rows), F32)], axis=1)
+    sides = jnp.transpose(jnp.concatenate([top, jnp.zeros((126, 256), F32)], axis=0))[0:rows]
+    tok_target = sides[:, 0:1].astype(jnp.int32)
+    tok_grad = sides[:, 1:2]
+
     def x_copy(h):
         return rcopy(gath.at[0, z, h], gath.at[1, z, h], x_send.at[h], x_recv.at[h], other_x, me_t)
 
@@ -140,12 +149,27 @@
         def _():
             t_copy(q, zz, h).start()
 
+    def late_x(r, h):
+        source = gath.at[0, me_t, h] if r == 0 else hb.at[0, r, h]
+        return rcopy(source, hb.at[1, r, h], w_send.at[r, h], w_recv.at[r, h], other_x, me_t)
+
+    def await_own(r, h):
+        rcopy(gath.at[0, 0, h], hb.at[0, r, h], t_send.at[0, 0, h], t_recv.at[0, r, h], me_v, tok_of(1)).wait_recv()
+
+    def late_others():
+        for h in LATE:
+            for r in range(1, 4):
+                await_own(r, h)
+                late_x(r, h).start()
+
+    distance = jnp.where(z > me_t, z - me_t, me_t - z)
     for h in range(CHUNKS):
         loads[h].wait()
+    for h in EARLY:
         x_copy(h).start()
     for s in range(depth):
-        for h in range(CHUNKS):
-            for q in range(2):
+        for h in ORDER:
+            for q in range(1 if h in LATE else 2):
                 if s == 0:
                     if q == 1:
                         x_copy(h).wait_recv()
@@ -180,9 +204,24 @@
 
                         pass_on(q, z + s, h)
 
-    for q in range(2):
-        for h in range(CHUNKS):
-            hb[q, 0, h] = gath[q, me_t, h]
+        @pl.when(distance == s)
+        def _():
+            for h in LATE:
+                late_x(0, h).start()
+
+        if s > 0:
+            @pl.when(distance == s - 1)
+            def _():
+                late_others()
+
+    @pl.when(distance == depth - 1)
+    def _():
+        late_others()
+
+    for h in range(CHUNKS):
+        hb[0, 0, h] = gath[0, me_t, h]
+    for h in EARLY:
+        hb[1, 0, h] = gath[1, me_t, h]
 
     def weight_rows(q):
         owner = (x + q) % 2
@@ -208,15 +247,19 @@
         return rcopy(cross_out, cross_in, c_send.at[0], c_recv.at[0], me_v, tok_of(2))
 
     def await_rel(r):
-        for q in range(2):
-            for h in range(CHUNKS):
-                rcopy(gath.at[q, 0, h], hb.at[q, r, h], t_send.at[q, 0, h], t_recv.at[q, r, h], me_v, tok_of(1)).wait_recv()
+        for h in EARLY:
+            if r > 0:
+                for q in range(2):
+                    rcopy(gath.at[q, 0, h], hb.at[q, r, h], t_send.at[q, 0, h], t_recv.at[q, r, h], me_v, tok_of(1)).wait_recv()
+        for h in LATE:
+            late_x(r, h).wait_recv()
 
     await_rel(2)
     await_rel(3)
     logits_of(2, 2)
     pair_copy(1).start()
     await_rel(1)
+    await_rel(0)
     logits_of(0, 2)
     pair_copy(0).start()
     pair_copy(1).wait_recv()
@@ -230,7 +273,7 @@
     masked = jnp.where(mask_ref[...] == 1, logits, jnp.float32(-1e30))
     local_max = jnp.max(masked, axis=1, keepdims=True)
     columns = me_v * width + lax.broadcasted_iota(jnp.int32, (rows, width), 1)
-    onehot = columns == targets_ref[...]
+    onehot = columns == tok_target
     local_target = jnp.sum(jnp.where(onehot, logits, 0.0), axis=1, keepdims=True)
     local_sum = jnp.sum(jnp.exp(masked - local_max), axis=1, keepdims=True)
     lanes = lax.broadcasted_iota(jnp.int32, (rows, 128), 1)
@@ -259,10 +302,10 @@
         denominator += got[1:2] * jnp.exp(got[0:1] - row_max)
         target_logit += got[2:3]
     log_norm = row_max + jnp.log(denominator)
-    loss_ref[...] = jnp.broadcast_to(log_norm - target_logit, loss_ref.shape)
+    loss_ref[...] = (log_norm - target_logit)[:, 0:rows]
     column = jnp.transpose(jnp.broadcast_to(log_norm, (128, 256)))[0:rows, 0:1]
     probabilities = jnp.exp(plog[0] - column)
-    dl[0] = (grad_ref[...] * (probabilities - onehot.astype(F32))).astype(BF)
+    dl[0] = (tok_grad * (probabilities - onehot.astype(F32))).astype(BF)
 
     def grad_copy(i):
         if i == 0:
@@ -279,28 +322,48 @@
             term_out.at[q, r, h], term_in.at[q, me_t, h], e_send.at[q, r, h], e_recv.at[q, r, h], me_v, tok_of(r)
         )
 
-    def terms_of(q, r0):
-        lhs = dl[pl.ds(r0, 2)].reshape(2 * rows, width)
+    def mix_copy(r, h):
+        return rcopy(mix_out.at[r, h], mix_in.at[r, h], m_send.at[r, h], m_recv.at[r, h], other_x, me_t)
+
+    def terms_of(q, r0, nr):
+        lhs = dl[pl.ds(r0, nr)].reshape(nr * rows, width)
         value = lax.dot_general(
             lhs, weight_ref[weight_rows(q), :], (((1,), (1,)), ((), ())), preferred_element_type=F32
-        ).astype(BF).reshape(2, CHUNKS, part, feats)
-        for i in range(2):
-            if r0 + i == 0:
-                term_in[q, me_t] = value[0]
-            else:
-                term_out[q, r0 + i] = value[i]
+        ).reshape(nr, CHUNKS, part, feats)
+        for i in range(nr):
+            r = r0 + i
+            for h in EARLY:
+                if r == 0:
+                    term_in[q, me_t, h] = value[i, h].astype(BF)
+                else:
+                    term_out[q, r, h] = value[i, h].astype(BF)
+                    term_copy(q, r, h).start()
+            for h in LATE:
+                if q == 0:
+                    near[r, h] = value[i, h]
+                else:
+                    mix_out[r, h] = value[i, h].astype(BF)
+                    mix_copy(r, h).start()
 
     grad_copy(1).wait_recv()
     for q in (1, 0):
-        terms_of(q, 0)
+        terms_of(q, 0, 2)
     grad_copy(0).wait_recv()
     grad_copy(2).start()
+    for q in (1, 0):
+        terms_of(q, 2, 1)
     grad_copy(2).wait_recv()
     for q in (1, 0):
-        terms_of(q, 2)
-        for h in range(CHUNKS):
-            for r in (2, 3, 1):
-                term_copy(q, r, h).start()
+        terms_of(q, 3, 1)
+    for r in range(4):
+        for h in LATE:
+            mix_copy(r, h).wait_recv()
+            both = (near[r, h] + mix_in[r, h].astype(F32)).astype(BF)
+            if r == 0:
+                term_in[0, me_t, h] = both
+            else:
+                term_out[0, r, h] = both
+                term_copy(0, r, h).start()
 
     def eu_copy(q, zz, h):
         return rcopy(up_out.at[q, zz, h], up_in.at[q, zz, h], eu_send.at[q, zz, h], eu_recv.at[q, zz, h], me_v + 2, me_t)
@@ -311,8 +374,9 @@
     def far_copy(h):
         return rcopy(far_out.at[h], far_in.at[h], f_send.at[h], f_recv.at[h], other_x, me_t)
 
-    for q in (1, 0):
-        for h in range(CHUNKS):
+    streams = [(q, h) for h in EARLY for q in (1, 0)] + [(0, h) for h in LATE]
+    for q, h in streams:
+        if True:
             for r in (1, 2, 3):
                 rcopy(term_out.at[q, r, h], term_in.at[q, tok_of(r), h], e_send.at[q, r, h], e_recv.at[q, r, h], me_v, tok_of(r)).wait_recv()
             for k in range(depth - 1, 0, -1):
@@ -350,8 +414,8 @@
 
                     ed_copy(q, zz, h).start()
 
-    for q in (1, 0):
-        for h in range(CHUNKS):
+    for q, h in streams:
+        if True:
             @pl.when(z > 0)
             def _():
                 eu_copy(q, z, h).wait_recv()
@@ -369,14 +433,21 @@
             if q == 1:
                 far_out[h] = total().astype(BF)
                 far_copy(h).start()
+            elif h in LATE:
+                out_ref[span(h), :] = total().astype(BF)
             else:
                 far_copy(h).wait_recv()
                 out_ref[span(h), :] = (total() + far_in[h].astype(F32)).astype(BF)
 
     for h in range(CHUNKS):
-        x_copy(h).wait_send()
-        far_copy(h).wait_send()
-        for q in range(2):
+        if h in EARLY:
+            x_copy(h).wait_send()
+            far_copy(h).wait_send()
+        else:
+            for r in range(4):
+                late_x(r, h).wait_send()
+                mix_copy(r, h).wait_send()
+        for q in range(1 if h in LATE else 2):
             for s in range(depth):
                 @pl.when(z - s >= 0)
                 def _():
@@ -429,7 +500,7 @@
             lambda *refs: kernel(depth, *refs),
             out_shape=(
                 jax.ShapeDtypeStruct((rows, feats), BF),
-                jax.ShapeDtypeStruct((8, 256), F32),
+                jax.ShapeDtypeStruct((1, rows), F32),
             ),
             in_specs=[pl.BlockSpec(memory_space=pltpu.HBM)] + [vmem] * 4,
             out_specs=(vmem, vmem),
@@ -451,18 +522,22 @@
                 pltpu.VMEM((2, depth) + block, BF),
                 pltpu.VMEM(block, BF),
                 pltpu.VMEM(block, BF),
+                pltpu.VMEM((4,) + block, F32),
+                pltpu.VMEM((4,) + block, BF),
+                pltpu.VMEM((4,) + block, BF),
                 dma((CHUNKS,)), dma((CHUNKS,)), dma((CHUNKS,)),
                 dma(by_q), dma(by_q), dma(by_q), dma(by_q), dma(by_q), dma(by_q),
                 dma((2,)), dma((2,)), dma((1,)), dma((1,)),
                 dma((vocab_size,)), dma((vocab_size,)), dma((3,)), dma((3,)),
                 dma(by_q), dma(by_q), dma(by_q), dma(by_q), dma(by_q), dma(by_q),
                 dma((CHUNKS,)), dma((CHUNKS,)),
+                dma((4, CHUNKS)), dma((4, CHUNKS)), dma((4, CHUNKS)), dma((4, CHUNKS)),
             ],
             compiler_params=pltpu.CompilerParams(
                 collective_id=0, has_side_effects=True, vmem_limit_bytes=60 * 1024 * 1024
             ),
-        )(hidden, head_weight, targets[:, None], vocab_mask[None, :], token_grad[:, None])
-        return (hidden_grad, loss[0, :rows])
+        )(hidden, head_weight, targets[None, :], vocab_mask[None, :], token_grad[None, :])
+        return (hidden_grad, loss.reshape(rows))
 
     return on_device
 

time: 167 us -> 152 us (0.910)
  Pallas kernels: 161 us -> 148 us
  local copies, waits for them, and re-layouts: 5.88 us -> 2.93 us
    pallas_call x1, Pallas kernels: 161 us -> 148 us  [on_device(): pl.pallas_call(lambda *refs: kernel(depth, *refs), out_shape=(jax.ShapeDt...]
    broadcast_in_dim x2 -> x0, local copies, waits for them, and re-layouts: 2.88 us -> none  [the longest x1 1.44 us: on_device(): targets[:, None]]
where the time goes in v3:
time: 152 us; the launch traced here: 151 us
  Pallas kernels  148 us (97%)
  local copies, waits for them, and re-layouts  2.93 us (2%)
    pallas_call x1, Pallas kernels, on_device(): pl.pallas_call(lambda *refs: kernel(depth, *refs), out_shape=(jax.ShapeDt...  148 us

profile of v3, /device:TPU:0, one launch (start us, length us, event | category | flops | bytes accessed | tf_op | source)
XLA Modules:
  0.0 151.4 jit_solution(4238914812129928647)
XLA Ops:
  0.6 147.8 %shard_map.68 = (bf16[192,896]{1,0:T(8,128)(2,1)}, f32[1,192]{1,0:T(1,128)}) custom-call(bf16[192,896]{1,0:T(8,128)(2,1)} %refs_0_.1, bf16[1792,1024]{1,0:T(8,128)(2,1)} %refs_1_.1, s32[1,192]{1,0:T(1,128)} %bitcast.5, s32[1,1024]{1,0:T(1,128)} %bitcast.4, f32[1,192]{1,0:T(1,128)} %bitcast.6), custom_call_target="tpu_custom_call" | custom-call | tf_op jit(solution)/shard_map/pallas_call | solution.py:499
  148.4 1.7 %copy.9 = bf16[192,896]{1,0:T(8,128)(2,1)} copy(bf16[192,896]{1,0:T(8,128)(2,1)} %get-tuple-element.8) | data formatting | bytes 688128
  150.2 1.2 copy.10

commit v4 on v3

--- a/solution.py
+++ b/solution.py
@@ -169,6 +169,22 @@
         x_copy(h).start()
     for s in range(depth):
         for h in ORDER:
+            if h == EARLY[0]:
+                @pl.when(distance == s)
+                def _():
+                    for late in LATE:
+                        late_x(0, late).start()
+
+                if s > 0:
+                    @pl.when(distance == s - 1)
+                    def _():
+                        late_others()
+
+                if s == depth - 1:
+                    @pl.when(distance == s)
+                    def _():
+                        late_others()
+
             for q in range(1 if h in LATE else 2):
                 if s == 0:
                     if q == 1:
@@ -204,20 +220,6 @@
 
                         pass_on(q, z + s, h)
 
-        @pl.when(distance == s)
-        def _():
-            for h in LATE:
-                late_x(0, h).start()
-
-        if s > 0:
-            @pl.when(distance == s - 1)
-            def _():
-                late_others()
-
-    @pl.when(distance == depth - 1)
-    def _():
-        late_others()
-
     for h in range(CHUNKS):
         hb[0, 0, h] = gath[0, me_t, h]
     for h in EARLY:
@@ -229,45 +231,63 @@
 
     tile = 256
 
-    def logits_of(r0, nr):
+    def logits_of(r0, nr, group):
+        c0, nc = len(LATE) * group, len((LATE, EARLY)[group])
+
         @pl.loop(0, width // tile)
         def _(j):
             cols = pl.ds(pl.multiple_of(j * tile, tile), tile)
             total = None
             for q in range(2):
-                lhs = hb[q, pl.ds(r0, nr)].reshape(nr * rows, feats)
+                lhs = hb[q, pl.ds(r0, nr), pl.ds(c0, nc)].reshape(nr * nc * part, feats)
                 term = jnp.dot(lhs, weight_ref[weight_rows(q), cols], preferred_element_type=F32)
                 total = term if total is None else total + term
-            plog[pl.ds(r0, nr), :, cols] = total.reshape(nr, rows, tile)
-
-    def pair_copy(k):
-        return rcopy(plog.at[1 + 2 * k], pair_in.at[k], p_send.at[k], p_recv.at[k], me_v, tok_of(1))
-
-    def cross_copy():
-        return rcopy(cross_out, cross_in, c_send.at[0], c_recv.at[0], me_v, tok_of(2))
-
-    def await_rel(r):
+            plog[pl.ds(r0, nr), pl.ds(c0 * part, nc * part), cols] = total.reshape(nr, nc * part, tile)
+
+    def group_rows(group):
+        return pl.ds(part * len(LATE) * group, part * len((LATE, EARLY)[group]))
+
+    def pair_copy(k, group):
+        return rcopy(
+            plog.at[1 + 2 * k, group_rows(group)], pair_in.at[k, group_rows(group)],
+            p_send.at[k, group], p_recv.at[k, group], me_v, tok_of(1),
+        )
+
+    def cross_copy(group):
+        return rcopy(
+            cross_out.at[group_rows(group)], cross_in.at[group_rows(group)],
+            c_send.at[group], c_recv.at[group], me_v, tok_of(2),
+        )
+
+    def cross_over(group):
+        pair_copy(1, group).wait_recv()
+        cross_out[group_rows(group), :] = plog[2, group_rows(group), :] + pair_in[1, group_rows(group), :]
+        cross_copy(group).start()
+
+    for r in range(1, 4):
         for h in EARLY:
-            if r > 0:
-                for q in range(2):
-                    rcopy(gath.at[q, 0, h], hb.at[q, r, h], t_send.at[q, 0, h], t_recv.at[q, r, h], me_v, tok_of(1)).wait_recv()
+            for q in range(2):
+                rcopy(gath.at[q, 0, h], hb.at[q, r, h], t_send.at[q, 0, h], t_recv.at[q, r, h], me_v, tok_of(1)).wait_recv()
+    logits_of(0, 4, 1)
+    pair_copy(1, 1).start()
+    pair_copy(0, 1).start()
+    cross_over(1)
+    for r in (2, 3):
         for h in LATE:
             late_x(r, h).wait_recv()
-
-    await_rel(2)
-    await_rel(3)
-    logits_of(2, 2)
-    pair_copy(1).start()
-    await_rel(1)
-    await_rel(0)
-    logits_of(0, 2)
-    pair_copy(0).start()
-    pair_copy(1).wait_recv()
-    cross_out[...] = plog[2] + pair_in[1]
-    cross_copy().start()
-    pair_copy(0).wait_recv()
+    logits_of(2, 2, 0)
+    pair_copy(1, 0).start()
+    cross_over(0)
+    for r in (0, 1):
+        for h in LATE:
+            late_x(r, h).wait_recv()
+    logits_of(0, 2, 0)
+    pair_copy(0, 0).start()
+    for group in (1, 0):
+        pair_copy(0, group).wait_recv()
     plog[0] = plog[0] + pair_in[0]
-    cross_copy().wait_recv()
+    for group in (1, 0):
+        cross_copy(group).wait_recv()
     logits = plog[0] + cross_in[...]
 
     masked = jnp.where(mask_ref[...] == 1, logits, jnp.float32(-1e30))
@@ -476,9 +496,10 @@
 
             for r in range(1, 4):
                 term_copy(q, r, h).wait_send()
-    for k in range(2):
-        pair_copy(k).wait_send()
-    cross_copy().wait_send()
+    for group in range(2):
+        for k in range(2):
+            pair_copy(k, group).wait_send()
+        cross_copy(group).wait_send()
     for k in range(1, nv):
         stat_copy(k).wait_send()
     for i in range(3):
@@ -527,7 +548,7 @@
                 pltpu.VMEM((4,) + block, BF),
                 dma((CHUNKS,)), dma((CHUNKS,)), dma((CHUNKS,)),
                 dma(by_q), dma(by_q), dma(by_q), dma(by_q), dma(by_q), dma(by_q),
-                dma((2,)), dma((2,)), dma((1,)), dma((1,)),
+                dma((2, 2)), dma((2, 2)), dma((2,)), dma((2,)),
                 dma((vocab_size,)), dma((vocab_size,)), dma((3,)), dma((3,)),
                 dma(by_q), dma(by_q), dma(by_q), dma(by_q), dma(by_q), dma(by_q),
                 dma((CHUNKS,)), dma((CHUNKS,)),

time: 152 us -> 140 us (0.921)
  Pallas kernels: 148 us -> 137 us
    pallas_call x1, Pallas kernels: 148 us -> 137 us  [on_device(): pl.pallas_call(lambda *refs: kernel(depth, *refs), out_shape=(jax.ShapeDt...]
where the time goes in v4:
time: 140 us
  Pallas kernels  137 us (98%)
  local copies, waits for them, and re-layouts  2.93 us (2%)
    pallas_call x1, Pallas kernels, on_device(): pl.pallas_call(lambda *refs: kernel(depth, *refs), out_shape=(jax.ShapeDt...  137 us
    unnamed x2, local copies, waits for them, and re-layouts  2.93 us

profile of v4, /device:TPU:0, one launch (start us, length us, event | category | flops | bytes accessed | tf_op | source)
XLA Modules:
  0.0 140.3 jit_solution(2310617605267895350)
XLA Ops:
  0.6 136.7 %shard_map.68 = (bf16[192,896]{1,0:T(8,128)(2,1)}, f32[1,192]{1,0:T(1,128)}) custom-call(bf16[192,896]{1,0:T(8,128)(2,1)} %refs_0_.1, bf16[1792,1024]{1,0:T(8,128)(2,1)} %refs_1_.1, s32[1,192]{1,0:T(1,128)} %bitcast.5, s32[1,1024]{1,0:T(1,128)} %bitcast.4, f32[1,192]{1,0:T(1,128)} %bitcast.6), custom_call_target="tpu_custom_call" | custom-call | tf_op jit(solution)/shard_map/pallas_call | solution.py:520
  137.4 1.7 %copy.9 = bf16[192,896]{1,0:T(8,128)(2,1)} copy(bf16[192,896]{1,0:T(8,128)(2,1)} %get-tuple-element.8) | data formatting | bytes 688128
  139.1 1.2 copy.10
